TPU v7x, 32 devices: a whole 2x2x4 slice. The times are simulated.
32 devices in a mesh: grp: 4 (over y, core), mem: 8 (over z, x).
Axes of the slice: x: 2, y: 2, z: 4, core: 2. Of those that a mesh axis runs over, the one named last changes fastest.
Arguments:
- factors: bfloat16 [64, 288, 1792], P(('grp', 'mem')), may hold values from -1.5 to 1.5
- screen: int32 [32, 18], P(('grp', 'mem')), may hold values from 0 to 1, as said below
Outputs:
- exchange_matrix: float32 [1792, 1792], P(('grp', 'mem'))
Inputs may be any that keep to these rules, and one draw needn't show every extreme that they name: screen[b, j] is 1 where auxiliary block b and occupied block j survive screening; every auxiliary block keeps at least one occupied block.
All inputs are finite; a program needn't handle non-finite values.
Results may differ from a plain program's by a relative error of at most 0.0003.
Values may be sent and summed in bfloat16 or wider, within the bound.
A program may use at most 128 MiB of HBM per device.

v0:
```python
import jax
import jax.numpy as jnp
from jax import lax
from jax.sharding import PartitionSpec as P


def on_device(factors, screen):
    aux_rows, occ_count, basis = factors.shape
    occ_blocks = screen.shape[1]
    occ_width = occ_count // occ_blocks
    blocks = factors.reshape(aux_rows, occ_blocks, occ_width, basis)
    kept_flag = screen[0]
    active = kept_flag == 1
    per_turn = max(1, 512 // (aux_rows * occ_width))
    active_int = active.astype(jnp.int32)
    block_order = jnp.argsort(1 - active_int, stable=True)
    block_order = jnp.concatenate([block_order, jnp.zeros((per_turn,), jnp.int32)])
    live_count = jnp.sum(active_int)
    turn_count = (live_count + per_turn - 1) // per_turn
    turn_slots = jnp.arange(per_turn, dtype=jnp.int32)
    groups = lax.axis_size("grp")
    members_all = lax.axis_size("mem")
    own_rows = basis // (groups * members_all)

    def add_turn(turn, running):
        picked = lax.dynamic_slice_in_dim(block_order, turn * per_turn, per_turn)
        weight = (turn * per_turn + turn_slots < live_count).astype(jnp.bfloat16)
        chosen = jnp.take(blocks, picked, axis=1) * weight[None, :, None, None]
        flat_rows = chosen.reshape(-1, basis)
        return running + lax.dot_general(
            flat_rows, flat_rows, (((0,), (0,)), ((), ())), preferred_element_type=jnp.float32
        )

    return lax.psum_scatter(
        lax.fori_loop(
            0,
            turn_count,
            add_turn,
            jnp.zeros((own_rows * lax.axis_size(("grp", "mem")), basis), jnp.float32),
        ),
        ("grp", "mem"),
        scatter_dimension=0,
        tiled=True,
    )


def solution(mesh):
    placed = (P(("grp", "mem"), None, None), P(("grp", "mem"), None))
    return jax.shard_map(
        on_device, mesh=mesh, in_specs=placed, out_specs=P(("grp", "mem"), None), check_vma=False
    )
```

profile of v0, /device:TPU:0, one launch (start us, length us, event | category | flops | bytes accessed | tf_op | source)
XLA Modules:
  0.0 326.3 jit_solution(4167648076849413669)
XLA Ops:
  6.5 0.0 reduce-scatter.2.cloned.1.call-start
  6.5 1.4 subtract_bitcast_fusion
  8.6 1.7 sort.17
  10.3 5.4 %broadcast_in_dim.16 = f32[1792,1792]{1,0:T(8,128)} broadcast(f32[]{:T(128)} %constant.42.clone.1), dimensions={} | broadcast | bytes 12845060 | tf_op jit(solution)/shard_map/broadcast_in_dim | solution.py:39
  15.8 12.7 %while.11 = (s32[]{:T(128)}, f32[1792,1792]{1,0:T(8,128)}, s32[]{:T(128)}, s32[34]{0:T(128)S(1)}, bf16[2,18,16,1792]{3,2,1,0:T(8,128)(2,1)}, /*index=5*/s32[]{:T(128)}, s32[]{:T(128)}, s32[]{:T(128)}, s32[]{:T(128)}, s32[]{:T(128)}) while((s32[]{:T(128)}, f32[1792,1792]{1,0:T(8,128)}, s32[]{:T(128)}, s32[34]{0:T(128)S(1)}, ...), condition=%wide.region_3.4_spmd.clone, body=%wide.region_2.3_spmd.clone.sunk | while | flops 3293381888 | bytes 31199744 | solution.py:35
  15.8 0.8 compare_and_fusion.2
  16.5 2.2 gather_fusion
  18.8 9.7 %bitcast_add_fusion.2 = f32[1792,1792]{1,0:T(8,128)} fusion(f32[1792,1792]{1,0:T(8,128)} %get-tuple-element.133, bf16[16,2,16,1792]{3,2,1,0:T(8,128)(2,1)S(1)} %gather_fusion, pred[16]{0:T(512)(128)(4,1)S(1)} %get-tuple-element.120, bf16[16]{0:T(256)(128)(2,1)S(1)} %get-tuple-element.121), kind=kOutput, calls=%fused_computation.2.clone.1 | convolution fusion | flops 3293380608 | bytes 27525168 | tf_op jit(solution)/shard_map/while/body/dot_general | solution.py:30
  28.5 0.0 reduce-scatter.2.cloned.1.call-update
  28.5 290.9 %reduce-scatter.2.cloned.1.call-done = f32[56,1792]{1,0:T(8,128)} async-done(((f32[1792,1792]{1,0:T(8,128)}), f32[56,1792]{1,0:T(8,128)}) %reduce-scatter.2.cloned.1.call-update) | async-done | bytes 401424 | tf_op jit(solution)/shard_map/reduce_scatter | solution.py:34
  (3 shorter events, 0.0 us)
Async XLA Ops:
  6.5 312.9 %reduce-scatter.2.cloned.1.call-start = ((), (), s32[]{:S(2)}) async-start(), calls=%async_computation.1 | async-start | bytes 13246464 | tf_op jit(solution)/shard_map/reduce_scatter | solution.py:34
Sparse Core Ops, SparseCore 0:
  28.7 290.7 reduce-scatter.1
where the time goes:
time: 327 us; the launch traced here: 326 us
  waiting for transfers between devices  291 us (89%)
  between operations  14.1 us (4%)
  matrix products  9.71 us (3%)
  local copies, waits for them, and re-layouts  7.68 us (2%)
  other arithmetic  3.84 us (1%)
    reduce_scatter x1, waiting for transfers between devices, on_device(): lax.psum_scatter(lax.fori_loop(0, turn_count, add_turn, jnp.zeros((own_ro...  291 us
    dot_general x1, matrix products, add_turn(): lax.dot_general(flat_rows, flat_rows, (((0,), (0,)), ((), ())), preferred...  9.71 us
  transfers between devices with their start and end apart: 1, of which 1 were waited for; matrix products, arithmetic and copies ran while one was open for 0% of the time, Pallas kernels for 0%

commit v1 on v0

v1 whole, which is shorter than its diff:
```python
import functools

import jax
import jax.numpy as jnp
from jax import lax
from jax.experimental import pallas as pl
from jax.experimental.pallas import tpu as pltpu
from jax.sharding import PartitionSpec as P

LANES = 128
TOP = 32767.0
MESH = pl.DeviceIdType.MESH


def bits_of(size):
    return size.bit_length() - 1


def orders_for(groups, members):
    near = [("mem", 1)]
    rows = [("grp", 2 << k) for k in range(bits_of(groups) - 1)]
    far = [("mem", 2 << k) for k in range(bits_of(members) - 1)]
    return near + rows + far, rows + near + far, far + near + rows


def kernel(
    groups, members, plan, chunks, width, x_ref, screen_ref, out_ref,
    both, turned, total, sent, got, sent_top, got_top, last,
    pair_send, pair_recv, data_send, data_recv, top_send, top_recv, end_send, end_recv,
):
    depth, basis = x_ref.shape
    own_rows = out_ref.shape[0]
    half = basis // 2
    occ_blocks = screen_ref.shape[1]
    grp, mem = lax.axis_index("grp"), lax.axis_index("mem")
    core = lax.rem(grp, 2)
    place = {"grp": grp, "mem": mem}
    levels = len(plan[0])
    starts = [0]
    for level in range(levels):
        starts.append(starts[-1] + (1 << (levels - 1 - level)))

    def peer(axis, step):
        bit = lax.rem(place[axis] // step, 2)
        there = place[axis] + (1 - 2 * bit) * step
        return (there, mem) if axis == "grp" else (grp, there)

    partner = peer("grp", 1)
    barrier = pltpu.get_barrier_semaphore()
    peers = [partner] + [peer(axis, step) for axis, step in plan[0]]
    for other in peers:
        pl.semaphore_signal(barrier, inc=1, device_id=other, device_id_type=MESH)


    def mask(j, carry):
        at = pl.ds(pl.multiple_of(j * width, width), width)
        keep = screen_ref[0, lax.rem(j, occ_blocks)].astype(jnp.float32)
        both[at, :] = (x_ref[at, :].astype(jnp.float32) * keep).astype(both.dtype)
        return carry

    pieces = 2
    piece = depth // pieces
    pair = []
    for n in range(pieces):
        lax.fori_loop(n * piece // width, (n + 1) * piece // width, mask, 0)
        if n == 0:
            pl.semaphore_wait(barrier, len(peers))
        pair.append(
            pltpu.make_async_remote_copy(
                src_ref=both.at[pl.ds(n * piece, piece)],
                dst_ref=both.at[pl.ds(depth + n * piece, piece)],
                send_sem=pair_send.at[n], recv_sem=pair_recv.at[n],
                device_id=partner, device_id_type=MESH,
            )
        )
        pair[-1].start()

    def turn(low, high):
        def one(m, carry):
            at = pl.ds(pl.multiple_of(m * 256, 256), 256)
            for k in range(low, high, LANES):
                turned[at, k : k + LANES] = both[k : k + LANES, at].T
            return carry

        lax.fori_loop(0, basis // 256, one, 0)

    early = depth // LANES * LANES
    turn(0, early)
    for copy in pair:
        copy.wait_recv()
    turn(early, 2 * depth)

    def rows_at(order, index):
        at = {"grp": grp - core, "mem": mem}
        for t, (axis, step) in enumerate(order):
            flip = index // (1 << (levels - 1 - t)) % 2
            bit = lax.rem(place[axis] // step, 2)
            at[axis] = at[axis] + flip * (1 - 2 * bit) * step
        first = (at["grp"] * members + at["mem"]) * own_rows
        second = first + members * own_rows
        return [pl.ds(pl.multiple_of(r, 8), own_rows) for r in (first, second)]

    def repeat(low, high, body):
        count = high - low
        by = 4 if count % 4 == 0 else count

        def step(t, carry):
            for u in range(by):
                body(low + t * by + u)
            return carry

        if count == by:
            step(0, 0)
        else:
            lax.fori_loop(0, count // by, step, 0)

    def columns(p):
        return slice(p * LANES, (p + 1) * LANES)

    def current(p, index, order):
        return jnp.concatenate([total[r, columns(p)] for r in rows_at(order, index)], axis=0)

    def arrived(p, level, index):
        top = got_top[p, level, pl.ds(index, 1), :]
        return got[p, starts[level] + index].astype(jnp.int32).astype(jnp.float32) * (top * (1.0 / TOP))

    def send(p, level):
        order = plan[p]
        count = 1 << (levels - 1 - level)

        def pack(i):
            value = current(p, count + i, order)
            if level:
                value = value + arrived(p, level - 1, count + i)
            top = jnp.max(jnp.abs(value), axis=0, keepdims=True)
            scale = TOP / jnp.maximum(top, 2e-34)
            sent[p, starts[level] + i] = jnp.round(value * scale).astype(jnp.int32).astype(jnp.int16)
            sent_top[p, level, pl.ds(i, 1), :] = top

        repeat(0, count, pack)
        to = peer(*order[level])
        run = pl.ds(starts[level], count)
        for here, there, a, b in (
            (sent.at[p, run], got.at[p, run], data_send, data_recv),
            (sent_top.at[p, level], got_top.at[p, level], top_send, top_recv),
        ):
            pltpu.make_async_remote_copy(
                src_ref=here, dst_ref=there, send_sem=a.at[p, level], recv_sem=b.at[p, level],
                device_id=to, device_id_type=MESH,
            ).start()

    def wait(p, level, done):
        run = pl.ds(starts[level], 1 << (levels - 1 - level))
        to = peer(*plan[p][level])
        for here, there, a, b in (
            (sent.at[p, run], got.at[p, run], data_send, data_recv),
            (sent_top.at[p, level], got_top.at[p, level], top_send, top_recv),
        ):
            copy = pltpu.make_async_remote_copy(
                src_ref=here, dst_ref=there, send_sem=a.at[p, level], recv_sem=b.at[p, level],
                device_id=to, device_id_type=MESH,
            )
            copy.wait_send() if done else copy.wait_recv()

    def keep(p, level):
        order = plan[p]

        def add(i):
            value = arrived(p, level, i)
            for n, r in enumerate(rows_at(order, i)):
                total[r, columns(p)] += value[n * own_rows : (n + 1) * own_rows]

        count = 1 << (levels - 1 - level)
        repeat(0, max(1, count // 2), add)

    parts = len(plan)
    part = 0
    for low, high in chunks:
        def multiply(m, carry):
            tall = basis // 2
            at = pl.ds(pl.multiple_of(m * tall, LANES), tall)
            total[at, low:high] = jnp.dot(
                turned[at, :],
                both[:, pl.ds(pl.multiple_of(core * half + low, LANES), high - low)],
                preferred_element_type=jnp.float32,
            )
            return carry

        lax.fori_loop(0, 2, multiply, 0)
        while part < high // LANES:
            send(part, 0)
            part += 1

    mine = pl.ds(pl.multiple_of((grp * members + mem) * own_rows, 8), own_rows)
    theirs = pl.ds(pl.multiple_of((partner[0] * members + mem) * own_rows, 8), own_rows)
    ends = []
    for level in range(levels):
        for p in range(parts):
            wait(p, level, False)
            if level + 1 < levels:
                send(p, level + 1)
            keep(p, level)
            if level + 1 == levels:
                at = pl.ds(pl.multiple_of(core * half + p * LANES, LANES), LANES)
                last[p] = total[theirs, columns(p)]
                copy = pltpu.make_async_remote_copy(
                    src_ref=last.at[p], dst_ref=out_ref.at[:, at],
                    send_sem=end_send.at[p], recv_sem=end_recv.at[p],
                    device_id=partner, device_id_type=MESH,
                )
                copy.start()
                ends.append(copy)
                out_ref[:, at] = total[mine, columns(p)]
    for copy in pair:
        copy.wait_send()
    for level in range(levels):
        for p in range(parts):
            wait(p, level, True)
    for copy in ends:
        copy.wait()


def solution(mesh):
    groups, members = mesh.shape["grp"], mesh.shape["mem"]

    def on_device(factors, screen):
        aux_rows, occ_count, basis = factors.shape
        depth = aux_rows * occ_count
        devices = groups * members
        real_rows = basis // devices
        own_rows = (real_rows + 7) // 8 * 8
        rows = factors.reshape(depth, basis)
        if own_rows != real_rows:
            rows = rows.reshape(depth, devices, real_rows)
            rows = jnp.pad(rows, ((0, 0), (0, 0), (0, own_rows - real_rows)))
            basis = devices * own_rows
            rows = rows.reshape(depth, basis)
        half = basis // 2
        parts = half // LANES
        first, second, third = orders_for(groups, members)
        plan = [(first, second, third, first, second, first, second)[p % 7] for p in range(parts)]
        chunks = [(low, min(low + 2 * LANES, half)) for low in range(0, half, 2 * LANES)]
        chips = groups * members // 2
        levels = bits_of(chips)
        block = 2 * own_rows
        places = max(8, chips // 2)
        dma = pltpu.SemaphoreType.DMA
        vmem = pl.BlockSpec(memory_space=pltpu.VMEM)
        result = pl.pallas_call(
            functools.partial(kernel, groups, members, plan, chunks, occ_count // screen.shape[1]),
            out_shape=jax.ShapeDtypeStruct((own_rows, basis), jnp.float32),
            in_specs=[vmem, pl.BlockSpec(memory_space=pltpu.SMEM)],
            out_specs=vmem,
            scratch_shapes=[
                pltpu.VMEM((2 * depth, basis), jnp.bfloat16),
                pltpu.VMEM((basis, 2 * depth), jnp.bfloat16),
                pltpu.VMEM((basis, half), jnp.float32),
                pltpu.VMEM((parts, chips - 1, block, LANES), jnp.int16),
                pltpu.VMEM((parts, chips - 1, block, LANES), jnp.int16),
                pltpu.VMEM((parts, levels, places, LANES), jnp.float32),
                pltpu.VMEM((parts, levels, places, LANES), jnp.float32),
                pltpu.VMEM((parts, own_rows, LANES), jnp.float32),
                dma((2,)), dma((2,)),
                dma((parts, levels)), dma((parts, levels)),
                dma((parts, levels)), dma((parts, levels)),
                dma((parts,)), dma((parts,)),
            ],
            compiler_params=pltpu.CompilerParams(
                collective_id=0, has_side_effects=True, vmem_limit_bytes=60 * 1024 * 1024
            ),
        )(rows, screen)
        if own_rows != real_rows:
            result = result[:real_rows].reshape(real_rows, devices, own_rows)[:, :, :real_rows]
            result = result.reshape(real_rows, devices * real_rows)
        return result

    placed = (P(("grp", "mem"), None, None), P(("grp", "mem"), None))
    return jax.shard_map(
        on_device, mesh=mesh, in_specs=placed, out_specs=P(("grp", "mem"), None), check_vma=False
    )
```

time: 327 us -> 54.5 us (0.17)
  waiting for transfers between devices: 291 us -> 0 us
  Pallas kernels: 0 us -> 52.6 us
  between operations: 14.1 us -> 0.01 us
  matrix products: 9.71 us -> 0 us
  local copies, waits for them, and re-layouts: 7.68 us -> 1.77 us
  other arithmetic: 3.84 us -> 0 us
    reduce_scatter x1 -> x0, waiting for transfers between devices: 291 us -> none  [on_device(): lax.psum_scatter(lax.fori_loop(0, turn_count, add_turn, jnp.zeros((own_ro...]
    pallas_call x0 -> x1, Pallas kernels: none -> 52.6 us  [on_device(): pl.pallas_call(functools.partial(kernel, groups, members, plan, chunks, o...]
    dot_general x1 -> x0, matrix products: 9.71 us -> none  [add_turn(): lax.dot_general(flat_rows, flat_rows, (((0,), (0,)), ((), ())), preferred...]
    broadcast_in_dim x1 -> x0, local copies, waits for them, and re-layouts: 5.43 us -> none  [on_device(): jnp.zeros((own_rows * lax.axis_size(('grp', 'mem')), basis), jnp.float32)]
  transfers between devices with their start and end apart: 1 -> 0, of which waited for: 1 -> 0; matrix products, arithmetic and copies ran while one was open for 0% -> 0% of each run, Pallas kernels for 0% -> 0%
where the time goes in v1:
time: 54.5 us; the launch traced here: 54.4 us
  Pallas kernels  52.6 us (97%)
  local copies, waits for them, and re-layouts  1.77 us (3%)
    pallas_call x1, Pallas kernels, on_device(): pl.pallas_call(functools.partial(kernel, groups, members, plan, chunks, o...  52.6 us
    unnamed x1, local copies, waits for them, and re-layouts  1.77 us

profile of v1, /device:TPU:0, one launch (start us, length us, event | category | flops | bytes accessed | tf_op | source)
XLA Modules:
  0.0 54.4 jit_solution(18364850192838528423)
XLA Ops:
  0.0 52.6 %shard_map.28 = f32[56,1792]{1,0:T(8,128)} custom-call(bf16[576,1792]{1,0:T(8,128)(2,1)} %bitcast.1, s32[1,18]{1,0:T(1,128)} %screen_ref.1), custom_call_target="tpu_custom_call" | custom-call | tf_op jit(solution)/shard_map/pallas_call | solution.py:249
  52.6 1.8 %copy.4 = f32[56,1792]{1,0:T(8,128)} copy(f32[56,1792]{1,0:T(8,128)} %shard_map.28) | data formatting | bytes 802816

commit v2 on v1

v2 whole, which is shorter than its diff:
```python
import functools

import jax
import jax.numpy as jnp
from jax import lax
from jax.experimental import pallas as pl
from jax.experimental.pallas import tpu as pltpu
from jax.sharding import PartitionSpec as P

LANES = 128
TOP = 32767.0
KINDS = "DGCFGFG"
STEPS = [0, 1, 2, 3, 4, 0, 1, 5, 6, 2, 3, 4, 0, 1, 5, 6]
MESH = pl.DeviceIdType.MESH


def bits_of(size):
    return size.bit_length() - 1


def plan_for(groups, members, parts):
    near = [[("mem", 1)]]
    rows = [[("grp", 2 << k)] for k in range(bits_of(groups) - 1)]
    far = [("mem", 2 << k) for k in range(bits_of(members) - 1)]
    single = [[bit] for bit in far]
    direct = [far[k : k + 2][::-1] for k in range(0, len(far), 2)]
    kinds = {
        "A": near + rows + direct,
        "B": rows + near + direct,
        "C": single + near + rows,
        "D": near + single + rows,
        "E": rows + single + near,
        "F": near + rows + single,
        "G": rows + near + single,
    }
    return [kinds[KINDS[p % len(KINDS)]] for p in range(parts)]


def messages_of(stages):
    left = 1
    for bits in stages:
        left <<= len(bits)
    result, slot = [], 0
    for level, bits in enumerate(stages):
        left >>= len(bits)
        for target in range(1, 1 << len(bits)):
            result.append((level, target, target * left, left, slot))
            slot += left
    return result


def kernel(
    groups, members, plan, chunks, width, x_ref, screen_ref, out_ref,
    both, turned, total, sent, got, sent_top, got_top, last,
    pair_send, pair_recv, data_send, data_recv, top_send, top_recv, end_send, end_recv,
):
    depth, basis = x_ref.shape
    own_rows = out_ref.shape[0]
    half = basis // 2
    occ_blocks = screen_ref.shape[1]
    grp, mem = lax.axis_index("grp"), lax.axis_index("mem")
    core = lax.rem(grp, 2)
    place = {"grp": grp, "mem": mem}
    def peer(bits):
        there = dict(place)
        for axis, step in bits:
            bit = lax.rem(place[axis] // step, 2)
            there[axis] = there[axis] + (1 - 2 * bit) * step
        return there["grp"], there["mem"]

    def chosen(bits, target):
        return tuple(b for t, b in enumerate(bits) if target >> (len(bits) - 1 - t) & 1)

    partner = peer([("grp", 1)])
    barrier = pltpu.get_barrier_semaphore()
    met = {
        tuple(sorted(chosen(stages[level], target)))
        for stages in plan
        for level, target, *_ in messages_of(stages)
    }
    peers = [partner] + [peer(bits) for bits in sorted(met)]
    for other in peers:
        pl.semaphore_signal(barrier, inc=1, device_id=other, device_id_type=MESH)


    def mask(j, carry):
        at = pl.ds(pl.multiple_of(j * width, width), width)
        keep = screen_ref[0, lax.rem(j, occ_blocks)].astype(jnp.float32)
        both[at, :] = (x_ref[at, :].astype(jnp.float32) * keep).astype(both.dtype)
        return carry

    pieces = 2
    piece = depth // pieces
    pair = []
    for n in range(pieces):
        lax.fori_loop(n * piece // width, (n + 1) * piece // width, mask, 0)
        if n == 0:
            pl.semaphore_wait(barrier, len(peers))
        pair.append(
            pltpu.make_async_remote_copy(
                src_ref=both.at[pl.ds(n * piece, piece)],
                dst_ref=both.at[pl.ds(depth + n * piece, piece)],
                send_sem=pair_send.at[n], recv_sem=pair_recv.at[n],
                device_id=partner, device_id_type=MESH,
            )
        )
        pair[-1].start()

    def turn(low, high):
        def one(m, carry):
            at = pl.ds(pl.multiple_of(m * 256, 256), 256)
            for k in range(low, high, LANES):
                turned[at, k : k + LANES] = both[k : k + LANES, at].T
            return carry

        lax.fori_loop(0, basis // 256, one, 0)

    early = depth // LANES * LANES
    turn(0, early)
    for copy in pair:
        copy.wait_recv()
    turn(early, 2 * depth)

    def rows_at(stages, index):
        order = [bit for bits in stages for bit in bits]
        at = {"grp": grp - core, "mem": mem}
        for t, (axis, step) in enumerate(order):
            flip = index // (1 << (len(order) - 1 - t)) % 2
            bit = lax.rem(place[axis] // step, 2)
            at[axis] = at[axis] + flip * (1 - 2 * bit) * step
        first = (at["grp"] * members + at["mem"]) * own_rows
        second = first + members * own_rows
        return [pl.ds(pl.multiple_of(r, 8), own_rows) for r in (first, second)]

    def repeat(low, high, body):
        count = high - low
        by = 4 if count % 4 == 0 else count

        def step(t, carry):
            for u in range(by):
                body(low + t * by + u)
            return carry

        if count == by:
            step(0, 0)
        else:
            lax.fori_loop(0, count // by, step, 0)

    def columns(p):
        return slice(p * LANES, (p + 1) * LANES)

    def current(p, index, order):
        return jnp.concatenate([total[r, columns(p)] for r in rows_at(order, index)], axis=0)

    def arrived(p, level, index):
        value = None
        for m, (at, _, _, _, slot) in enumerate(messages_of(plan[p])):
            if at == level:
                top = got_top[p, m, pl.ds(index, 1), :] * (1.0 / TOP)
                one = got[p, slot + index].astype(jnp.int32).astype(jnp.float32) * top
                value = one if value is None else value + one
        return value

    def copies(p, m):
        level, target, _, count, slot = messages_of(plan[p])[m]
        run = pl.ds(slot, count)
        to = peer(chosen(plan[p][level], target))
        return [
            pltpu.make_async_remote_copy(
                src_ref=here, dst_ref=there, send_sem=a.at[p, m], recv_sem=b.at[p, m],
                device_id=to, device_id_type=MESH,
            )
            for here, there, a, b in (
                (sent.at[p, run], got.at[p, run], data_send, data_recv),
                (sent_top.at[p, m], got_top.at[p, m], top_send, top_recv),
            )
        ]

    def send(p, level):
        for m, (at, _, first, count, slot) in reversed(list(enumerate(messages_of(plan[p])))):
            if at != level:
                continue

            def pack(i):
                value = current(p, first + i, plan[p])
                if level:
                    value = value + arrived(p, level - 1, first + i)
                top = jnp.max(jnp.abs(value), axis=0, keepdims=True)
                scale = TOP / jnp.maximum(top, 2e-34)
                sent[p, slot + i] = jnp.round(value * scale).astype(jnp.int32).astype(jnp.int16)
                sent_top[p, m, pl.ds(i, 1), :] = top

            repeat(0, count, pack)
            for copy in copies(p, m):
                copy.start()

    def wait(p, level):
        for m, (at, *_) in enumerate(messages_of(plan[p])):
            if at == level:
                for copy in copies(p, m):
                    copy.wait_recv()

    def keep(p, level):
        count = [n for at, _, _, n, _ in messages_of(plan[p]) if at == level][0]
        if level + 1 < len(plan[p]):
            count >>= len(plan[p][level + 1])

        def add(i):
            value = arrived(p, level, i)
            for n, r in enumerate(rows_at(plan[p], i)):
                total[r, columns(p)] += value[n * own_rows : (n + 1) * own_rows]

        repeat(0, count, add)

    parts = len(plan)
    mine = pl.ds(pl.multiple_of((grp * members + mem) * own_rows, 8), own_rows)
    theirs = pl.ds(pl.multiple_of((partner[0] * members + mem) * own_rows, 8), own_rows)
    ends = []

    def advance(p, level):
        wait(p, level)
        if level + 1 < len(plan[p]):
            send(p, level + 1)
            keep(p, level)
            return
        keep(p, level)
        last[p] = total[theirs, columns(p)]
        at = pl.ds(pl.multiple_of(core * half + p * LANES, LANES), LANES)
        copy = pltpu.make_async_remote_copy(
            src_ref=last.at[p], dst_ref=out_ref.at[:, at],
            send_sem=end_send.at[p], recv_sem=end_recv.at[p],
            device_id=partner, device_id_type=MESH,
        )
        copy.start()
        ends.append(copy)
        out_ref[:, at] = total[mine, columns(p)]

    def multiply(low, high):
        def one(m, carry):
            tall = basis // 2
            at = pl.ds(pl.multiple_of(m * tall, LANES), tall)
            total[at, low:high] = jnp.dot(
                turned[at, :],
                both[:, pl.ds(pl.multiple_of(core * half + low, LANES), high - low)],
                preferred_element_type=jnp.float32,
            )
            return carry

        lax.fori_loop(0, 2, one, 0)

    step = [0] * parts
    made = 0
    for p in STEPS + list(range(parts)) * (2 + max(len(stages) for stages in plan)):
        if p >= parts or step[p] > len(plan[p]):
            continue
        if step[p] == 0:
            while chunks[made][0] <= p * LANES if made < len(chunks) else False:
                multiply(*chunks[made])
                made += 1
            send(p, 0)
        else:
            advance(p, step[p] - 1)
        step[p] += 1
    for copy in pair:
        copy.wait_send()
    for p in range(parts):
        for m in range(len(messages_of(plan[p]))):
            for copy in copies(p, m):
                copy.wait_send()
    for copy in ends:
        copy.wait()


def solution(mesh):
    groups, members = mesh.shape["grp"], mesh.shape["mem"]

    def on_device(factors, screen):
        aux_rows, occ_count, basis = factors.shape
        depth = aux_rows * occ_count
        devices = groups * members
        real_rows = basis // devices
        own_rows = (real_rows + 7) // 8 * 8
        rows = factors.reshape(depth, basis)
        if own_rows != real_rows:
            rows = rows.reshape(depth, devices, real_rows)
            rows = jnp.pad(rows, ((0, 0), (0, 0), (0, own_rows - real_rows)))
            basis = devices * own_rows
            rows = rows.reshape(depth, basis)
        half = basis // 2
        parts = half // LANES
        plan = plan_for(groups, members, parts)
        chunks = [(low, min(low + 2 * LANES, half)) for low in range(0, half, 2 * LANES)]
        chips = groups * members // 2
        levels = max(len(messages_of(stages)) for stages in plan)
        block = 2 * own_rows
        places = max(8, chips // 2)
        dma = pltpu.SemaphoreType.DMA
        vmem = pl.BlockSpec(memory_space=pltpu.VMEM)
        result = pl.pallas_call(
            functools.partial(kernel, groups, members, plan, chunks, occ_count // screen.shape[1]),
            out_shape=pltpu.VMEM((own_rows, basis), jnp.float32),
            in_specs=[vmem, pl.BlockSpec(memory_space=pltpu.SMEM)],
            out_specs=vmem,
            scratch_shapes=[
                pltpu.VMEM((2 * depth, basis), jnp.bfloat16),
                pltpu.VMEM((basis, 2 * depth), jnp.bfloat16),
                pltpu.VMEM((basis, half), jnp.float32),
                pltpu.VMEM((parts, chips - 1, block, LANES), jnp.int16),
                pltpu.VMEM((parts, chips - 1, block, LANES), jnp.int16),
                pltpu.VMEM((parts, levels, places, LANES), jnp.float32),
                pltpu.VMEM((parts, levels, places, LANES), jnp.float32),
                pltpu.VMEM((parts, own_rows, LANES), jnp.float32),
                dma((2,)), dma((2,)),
                dma((parts, levels)), dma((parts, levels)),
                dma((parts, levels)), dma((parts, levels)),
                dma((parts,)), dma((parts,)),
            ],
            compiler_params=pltpu.CompilerParams(
                collective_id=0, has_side_effects=True, vmem_limit_bytes=60 * 1024 * 1024
            ),
        )(rows, screen)
        if own_rows != real_rows:
            result = result[:real_rows].reshape(real_rows, devices, own_rows)[:, :, :real_rows]
            result = result.reshape(real_rows, devices * real_rows)
        return result

    placed = (P(("grp", "mem"), None, None), P(("grp", "mem"), None))
    return jax.shard_map(
        on_device, mesh=mesh, in_specs=placed, out_specs=P(("grp", "mem"), None), check_vma=False
    )
```

time: 54.5 us -> 49.5 us (0.908)
  Pallas kernels: 52.6 us -> 48.6 us
  local copies, waits for them, and re-layouts: 1.77 us -> 0.75 us
    pallas_call x1, Pallas kernels: 52.6 us -> 48.6 us  [on_device(): pl.pallas_call(functools.partial(kernel, groups, members, plan, chunks, o...]
    unnamed x1, local copies, waits for them, and re-layouts: 1.77 us -> 0.75 us
where the time goes in v2:
time: 49.5 us; the launch traced here: 49.4 us
  Pallas kernels  48.6 us (98%)
  local copies, waits for them, and re-layouts  0.75 us (2%)
    pallas_call x1, Pallas kernels, on_device(): pl.pallas_call(functools.partial(kernel, groups, members, plan, chunks, o...  48.6 us

profile of v2, /device:TPU:0, one launch (start us, length us, event | category | flops | bytes accessed | tf_op | source)
XLA Modules:
  0.0 49.4 jit_solution(14540535207378269747)
XLA Ops:
  0.0 48.6 %shard_map.28 = f32[56,1792]{1,0:T(8,128)S(1)} custom-call(bf16[576,1792]{1,0:T(8,128)(2,1)} %bitcast.1, s32[1,18]{1,0:T(1,128)} %screen_ref.1), custom_call_target="tpu_custom_call" | custom-call | tf_op jit(solution)/shard_map/pallas_call | solution.py:299
  48.6 0.8 %copy.4 = f32[56,1792]{1,0:T(8,128)} copy(f32[56,1792]{1,0:T(8,128)S(1)} %shard_map.28) | data formatting | bytes 802816
